TPU v7x, 256 devices: a whole 4x4x8 slice. The times are simulated.
256 devices in a mesh: node: 32 (over x, z_hi, core), local: 8 (over z_lo, y).
Axes of the slice: x: 4, y: 4, z: 8 (z_hi: 4, z_lo: 2; z = z_hi * 2 + z_lo), core: 2. Of those that a mesh axis runs over, the one named last changes fastest.
Arguments:
- hidden: bfloat16 [8, 8192, 4096], P('local', 'node'), may hold values from -6 to 6
- queries: bfloat16 [8, 8192, 2048], P('local', 'node'), may hold values from -30 to 30
- saved_keys: bfloat16 [8, 8192, 512], P('local', 'node'), may hold values from -30 to 30
- grad_out: bfloat16 [8, 8192, 2048], P('local', 'node'), may hold values from -6 to 6
- value_weight: bfloat16 [4096, 512], P('local'), may hold values from -0.09375 to 0.09375
- doc_lengths: int32 [8, 32], P('local'), may hold values from 0 to 1024, as said below
- doc_order: int32 [8, 32], P('local'), may hold values from 0 to 31, each once within a row
Outputs:
- query_grad: bfloat16 [8, 8192, 2048], P('local', 'node')
- key_grad: bfloat16 [8, 8192, 512], P('local', 'node')
- input_grad: bfloat16 [8, 8192, 4096], P('local', 'node')
- weight_grad: float32 [4096, 512], P(('node', 'local'))
Inputs may be any that keep to these rules, and one draw needn't show every extreme that they name: `doc_lengths`: a document occupies ceil(length / 256) whole blocks, at most 4; the documents of a sequence fill its 32 blocks exactly; in every sequence some document takes 4 blocks.
All inputs are finite; a program needn't handle non-finite values.
Results may differ from a plain program's by a relative error of at most 0.0085.
Values may be sent and summed in bfloat16 or wider, within the bound.
No kernel may reach another device: no remote copies, remote signals or barrier semaphores. Data moves between devices by JAX's collectives and lax.ppermute only.
A program may use at most 128 MiB of HBM per device.

v0:
```python
import jax
import jax.numpy as jnp
from jax import lax
from jax.sharding import PartitionSpec as P

HD = 128
DOCB = 4


masked_score = -1e30


def from_behind(block, axis, distance):
    devices = range(lax.axis_size(axis))
    route = [(i - distance, i) for i in devices if i - distance in devices]
    return lax.ppermute(block, axis, route)


def in_blocks(array, dim, count):
    before, after = (array.shape[:dim], array.shape[dim + 1 :])
    return jnp.moveaxis(array.reshape(*before, count, -1, *after), dim, 0)


def sent_and_summed(array, axis, dim):
    pieces = in_blocks(array, dim, lax.axis_size(axis))
    arrived = lax.all_to_all(pieces, axis, split_axis=0, concat_axis=0, tiled=True)
    return arrived.astype(jnp.float32).sum(axis=0)


def summed_on_arrival(array, axis, dim):
    pieces = in_blocks(array, dim, lax.axis_size(axis))
    arrived = lax.all_to_all(pieces, axis, split_axis=0, concat_axis=0, tiled=True)
    return arrived.sum(axis=0)


def doc_layout(lengths_row, order_row, block_rows):
    slot_total = lengths_row.shape[0]
    slot_ids = jnp.arange(slot_total, dtype=jnp.int32)
    picked = order_row[:, None] == slot_ids[None, :]
    lens_ord = jnp.sum(jnp.where(picked, lengths_row[None, :], 0), axis=1)
    block_count = (lens_ord + block_rows - 1) // block_rows
    first_block = jnp.cumsum(block_count) - block_count
    return (lens_ord, block_count, first_block)


def block_info(block_index, lens_ord, block_count, first_block):
    member = (first_block <= block_index) & (block_index < first_block + block_count)
    has_doc = jnp.any(member)
    doc_start = jnp.sum(jnp.where(member, first_block, 0))
    length = jnp.sum(jnp.where(member, lens_ord, 0))
    return (jnp.where(has_doc, doc_start, -1), length)


def window_mask(block_index, layout, block_rows):
    doc_start, length = block_info(block_index, *layout)
    inside = jnp.arange(block_rows, dtype=jnp.int32)
    query_ok = (block_index - doc_start) * block_rows + inside < length
    mask_parts = []
    for offset in range(DOCB - 1, -1, -1):
        other_block = block_index - offset
        other_start, other_len = block_info(other_block, *layout)
        key_ok = (other_start == doc_start) & (
            (other_block - doc_start) * block_rows + inside < length
        )
        allowed = jnp.broadcast_to(key_ok[None, :], (block_rows, block_rows))
        if offset == 0:
            allowed = allowed & (inside[None, :] <= inside[:, None])
        mask_parts.append(allowed)
    return (query_ok, jnp.concatenate(mask_parts, axis=1), doc_start)


def window_grads(query_rows, grad_rows, key_window, value_window, allowed):
    row_count = query_rows.shape[0]
    kv_heads = key_window.shape[1] // HD
    group = query_rows.shape[1] // key_window.shape[1]
    score_scale = HD ** (-0.5)
    query_parts, key_parts, value_parts = ([], [], [])
    for kv_head in range(kv_heads):
        low_col = kv_head * group * HD
        high_col = (kv_head + 1) * group * HD
        q_cols = query_rows[:, low_col:high_col].reshape(row_count, group, HD)
        g_cols = grad_rows[:, low_col:high_col].reshape(row_count, group, HD)
        k_cols = key_window[:, kv_head * HD : (kv_head + 1) * HD]
        v_cols = value_window[:, kv_head * HD : (kv_head + 1) * HD]
        scores = (
            jnp.einsum("tjd,wd->jtw", q_cols, k_cols, preferred_element_type=jnp.float32)
            * score_scale
        )
        scores = jnp.where(allowed[None], scores, masked_score)
        peak = jnp.max(scores, axis=2, keepdims=True)
        expd = jnp.exp(scores - peak)
        attn_probs = expd / jnp.sum(expd, axis=2, keepdims=True)
        attn_low = attn_probs.astype(jnp.bfloat16)
        attn_out = jnp.einsum("jtw,wd->tjd", attn_low, v_cols, preferred_element_type=jnp.float32)
        prob_grad = jnp.einsum("tjd,wd->jtw", g_cols, v_cols, preferred_element_type=jnp.float32)
        row_delta = jnp.einsum("tjd,tjd->jt", g_cols.astype(jnp.float32), attn_out)
        score_grad = (attn_probs * (prob_grad - row_delta[:, :, None]) * score_scale).astype(
            jnp.bfloat16
        )
        head_query = jnp.einsum(
            "jtw,wd->tjd", score_grad, k_cols, preferred_element_type=jnp.float32
        )
        query_parts.append(head_query.astype(jnp.bfloat16).reshape(row_count, group * HD))
        key_parts.append(
            jnp.einsum("jtw,tjd->wd", score_grad, q_cols, preferred_element_type=jnp.float32)
        )
        value_parts.append(
            jnp.einsum("jtw,tjd->wd", attn_low, g_cols, preferred_element_type=jnp.float32)
        )
    key_grad = jnp.concatenate(key_parts, axis=1)
    value_grad = jnp.concatenate(value_parts, axis=1)
    return (jnp.concatenate(query_parts, axis=1), key_grad, value_grad)


def local(hidden, queries, saved_keys, grad_out, value_weight, doc_lengths, doc_order):
    block_index = lax.axis_index("node")
    x_rows = hidden[0]
    query_rows = queries[0]
    key_rows = saved_keys[0]
    row_count = x_rows.shape[0]
    layout = doc_layout(doc_lengths[0], doc_order[0], row_count)
    query_ok, allowed, doc_start = window_mask(block_index, layout, row_count)
    grad_rows = grad_out[0] * query_ok[:, None].astype(jnp.bfloat16)
    full_weight = lax.all_gather(value_weight, "local", axis=0, tiled=True)
    values = jnp.dot(x_rows, full_weight, preferred_element_type=jnp.float32).astype(jnp.bfloat16)
    key_list = [key_rows]
    value_list = [values]
    for offset in range(1, DOCB):
        earlier_key, earlier_value = from_behind((key_rows, values), "node", offset)
        key_list.insert(0, earlier_key)
        value_list.insert(0, earlier_value)
    key_window = jnp.concatenate(key_list, axis=0)
    value_window = jnp.concatenate(value_list, axis=0)
    query_grad, key_win, value_win = window_grads(
        query_rows, grad_rows, key_window, value_window, allowed
    )
    own_low = (DOCB - 1) * row_count
    key_total = key_win[own_low:]
    value_total = value_win[own_low:]
    for offset in range(1, DOCB):
        low_row = (DOCB - 1 - offset) * row_count
        key_piece = key_win[low_row : low_row + row_count]
        value_piece = value_win[low_row : low_row + row_count]
        got_key, got_value = (
            from_behind(key_piece.astype(jnp.bfloat16), "node", -offset).astype(key_piece.dtype),
            from_behind(value_piece.astype(jnp.bfloat16), "node", -offset).astype(
                value_piece.dtype
            ),
        )
        key_total = key_total + got_key
        value_total = value_total + got_value
    value_low = value_total.astype(jnp.bfloat16)
    contract_cols = (((1,), (1,)), ((), ()))
    input_grad = lax.dot_general(
        value_low, full_weight, contract_cols, preferred_element_type=jnp.float32
    )
    node_part = sent_and_summed(
        lax.dot_general(
            x_rows, value_low, (((0,), (0,)), ((), ())), preferred_element_type=jnp.float32
        ).astype(jnp.bfloat16),
        "node",
        0,
    )
    weight_grad = summed_on_arrival(node_part, "local", 0)
    return (
        query_grad[None],
        key_total.astype(jnp.bfloat16)[None],
        input_grad.astype(jnp.bfloat16)[None],
        weight_grad,
    )


def solution(mesh):
    placed = (
        P("local", "node", None),
        P("local", "node", None),
        P("local", "node", None),
        P("local", "node", None),
        P("local", None),
        P("local", None),
        P("local", None),
    )
    return jax.shard_map(
        local,
        mesh=mesh,
        in_specs=placed,
        out_specs=(
            P("local", "node", None),
            P("local", "node", None),
            P("local", "node", None),
            P(("node", "local"), None),
        ),
        check_vma=False,
    )
```

profile of v0, /device:TPU:2, one launch (start us, length us, event | category | flops | bytes accessed | tf_op | source)
XLA Modules:
  0.0 336.5 jit_solution(3093472141666664696)
XLA Ops:
  9.3 5.2 %collective-permute-start.1 = (bf16[256,512]{1,0:T(8,128)(2,1)}, bf16[256,512]{1,0:T(8,128)(2,1)}, u32[]{:S(2)}, u32[]{:S(2)}) collective-permute-start(bf16[256,512]{1,0:T(8,128)(2,1)} %bitcast.329), channel_id=1, source_target_pairs={{0,16},{8,24},{16,32},{24,40},{32,48},{40,56},{48,64},{56,72},{64,... | collective-permute-start | bytes 786440 | tf_op jit(solution)/shard_map/ppermute | solution.py:16
  14.5 7.3 %collective-permute-start = (bf16[256,512]{1,0:T(8,128)(2,1)}, bf16[256,512]{1,0:T(8,128)(2,1)}, u32[]{:S(2)}, u32[]{:S(2)}) collective-permute-start(bf16[256,512]{1,0:T(8,128)(2,1)} %bitcast.330), channel_id=1, source_target_pairs={{0,24},{8,32},{16,40},{24,48},{32,56},{40,64},{48,72},{56,80},{64,... | collective-permute-start | bytes 786440 | tf_op jit(solution)/shard_map/ppermute | solution.py:16
  37.4 10.4 %collective-permute-done = bf16[256,512]{1,0:T(8,128)(2,1)} collective-permute-done((bf16[256,512]{1,0:T(8,128)(2,1)}, bf16[256,512]{1,0:T(8,128)(2,1)}, u32[]{:S(2)}, u32[]{:S(2)}) %collective-permute-start) | collective-permute-done | bytes 262176 | tf_op jit(solution)/shard_map/ppermute | solution.py:16
  49.0 4.8 %fusion.92 = (f32[4,256]{1,0:T(4,128)S(1)}, f32[4,256,1024]{1,2,0:T(8,128)}) fusion(pred[256,1024]{0,1:T(8,128)(4,1)} %pad_add_fusion, bf16[256,4,128]{0,2,1:T(8,128)(2,1)} %bitcast.326, bf16[1024,512]{1,0:T(8,128)(2,1)S(1)} %pad_maximum_fusion.2), kind=kOutput, calls=%fused_computation.164 | convolution fusion | flops 272630784 | bytes 4984832 | tf_op jit(solution)/shard_map/sub | solution.py:91
  58.6 4.6 %fusion.95 = (f32[4,256]{1,0:T(4,128)S(1)}, f32[4,256,1024]{1,2,0:T(8,128)}) fusion(pred[256,1024]{0,1:T(8,128)(4,1)} %pad_add_fusion, bf16[256,4,128]{0,2,1:T(8,128)(2,1)S(1)} %bitcast.325, bf16[1024,512]{1,0:T(8,128)(2,1)} %copy-done.21), kind=kOutput, calls=%fused_computation.167 | convolution fusion | flops 272630784 | bytes 4984832 | tf_op jit(solution)/shard_map/sub | solution.py:91
  67.9 4.6 %fusion.93 = (f32[4,256]{1,0:T(4,128)S(1)}, f32[4,256,1024]{1,2,0:T(8,128)}) fusion(pred[256,1024]{0,1:T(8,128)(4,1)} %pad_add_fusion, bf16[256,4,128]{0,2,1:T(8,128)(2,1)} %bitcast.322, bf16[1024,512]{1,0:T(8,128)(2,1)} %copy-done.21), kind=kOutput, calls=%fused_computation.165 | convolution fusion | flops 272630784 | bytes 4984832 | tf_op jit(solution)/shard_map/sub | solution.py:91
  78.1 4.6 %fusion.94 = (f32[4,256]{1,0:T(4,128)S(1)}, f32[4,256,1024]{1,2,0:T(8,128)}) fusion(pred[256,1024]{0,1:T(8,128)(4,1)} %pad_add_fusion, bf16[256,4,128]{0,2,1:T(8,128)(2,1)} %bitcast.320, bf16[1024,512]{1,0:T(8,128)(2,1)} %copy-done.21), kind=kOutput, calls=%fused_computation.166 | convolution fusion | flops 272630784 | bytes 4984832 | tf_op jit(solution)/shard_map/sub | solution.py:91
  88.8 5.4 %collective-permute-start.11 = (bf16[256,512]{0,1:T(8,128)(2,1)S(1)}, bf16[256,512]{0,1:T(8,128)(2,1)S(1)}, u32[]{:S(2)}, u32[]{:S(2)}) collective-permute-start(bf16[256,512]{0,1:T(8,128)(2,1)S(1)} %get-tuple-element.37), channel_id=1, source_target_pairs={{24,0},{32,8},{40,16},{48,24},{56,32},{64,40},{72,48},{80,56},{88,... | collective-permute-start | bytes 786440 | tf_op jit(solution)/shard_map/ppermute | solution.py:16
  94.2 4.9 %collective-permute-start.10 = (bf16[256,512]{0,1:T(8,128)(2,1)S(1)}, bf16[256,512]{0,1:T(8,128)(2,1)S(1)}, u32[]{:S(2)}, u32[]{:S(2)}) collective-permute-start(bf16[256,512]{0,1:T(8,128)(2,1)S(1)} %get-tuple-element.38), channel_id=1, source_target_pairs={{16,0},{24,8},{32,16},{40,24},{48,32},{56,40},{64,48},{72,56},{80,... | collective-permute-start | bytes 786440 | tf_op jit(solution)/shard_map/ppermute | solution.py:16
  99.3 10.0 %collective-permute-done.9 = bf16[256,512]{0,1:T(8,128)(2,1)S(1)} collective-permute-done((bf16[256,512]{0,1:T(8,128)(2,1)S(1)}, bf16[256,512]{0,1:T(8,128)(2,1)S(1)}, u32[]{:S(2)}, u32[]{:S(2)}) %collective-permute-start.9) | collective-permute-done | bytes 262176 | tf_op jit(solution)/shard_map/ppermute | solution.py:16
  112.1 4.3 %collective-permute-done.10 = bf16[256,512]{0,1:T(8,128)(2,1)S(1)} collective-permute-done((bf16[256,512]{0,1:T(8,128)(2,1)S(1)}, bf16[256,512]{0,1:T(8,128)(2,1)S(1)}, u32[]{:S(2)}, u32[]{:S(2)}) %collective-permute-start.10) | collective-permute-done | bytes 262176 | tf_op jit(solution)/shard_map/ppermute | solution.py:16
  117.8 3.2 copy.272
  121.0 9.2 %all-to-all-start = ((bf16[32,128,512]{1,2,0:T(8,128)(2,1)}), bf16[32,128,512]{1,2,0:T(8,128)(2,1)}, u32[]{:S(2)}, u32[]{:S(2)}) async-start(bf16[32,128,512]{1,2,0:T(8,128)(2,1)} %bitcast.302), calls=%async_computation | async-start | bytes 8388608 | tf_op jit(solution)/shard_map/all_to_all | solution.py:26
  130.2 3.6 %fusion.45 = bf16[256,512]{1,0:T(8,128)(2,1)S(1)} fusion(bf16[4096,512]{1,0:T(8,128)(2,1)} %all-gather.2.cloned.1.call-done, bf16[1,256,4096]{2,1,0:T(8,128)(2,1)S(1)} %copy-done), kind=kOutput, calls=%fused_computation.79 | convolution fusion | flops 1073872896 | bytes 6553600 | tf_op jit(solution)/shard_map/dot_general | solution.py:125
  135.8 4.3 %collective-permute-start.4 = (bf16[256,512]{1,0:T(8,128)(2,1)S(1)}, bf16[256,512]{1,0:T(8,128)(2,1)S(1)}, u32[]{:S(2)}, u32[]{:S(2)}) collective-permute-start(bf16[256,512]{1,0:T(8,128)(2,1)S(1)} %fusion.45), channel_id=1, source_target_pairs={{0,16},{8,24},{16,32},{24,40},{32,48},{40,56},{48,64},{56,72},{64,... | collective-permute-start | bytes 786440 | tf_op jit(solution)/shard_map/ppermute | solution.py:16
  140.1 5.4 %collective-permute-start.3 = (bf16[256,512]{1,0:T(8,128)(2,1)S(1)}, bf16[256,512]{1,0:T(8,128)(2,1)S(1)}, u32[]{:S(2)}, u32[]{:S(2)}) collective-permute-start(bf16[256,512]{1,0:T(8,128)(2,1)S(1)} %fusion.45), channel_id=1, source_target_pairs={{0,24},{8,32},{16,40},{24,48},{32,56},{40,64},{48,72},{56,80},{64,... | collective-permute-start | bytes 786440 | tf_op jit(solution)/shard_map/ppermute | solution.py:16
  148.1 92.2 %collective-permute-done.5 = bf16[256,512]{1,0:T(8,128)(2,1)S(1)} collective-permute-done((bf16[256,512]{1,0:T(8,128)(2,1)S(1)}, bf16[256,512]{1,0:T(8,128)(2,1)S(1)}, u32[]{:S(2)}, u32[]{:S(2)}) %collective-permute-start.5) | collective-permute-done | bytes 262176 | tf_op jit(solution)/shard_map/ppermute | solution.py:16
  241.3 11.0 %collective-permute-done.3 = bf16[256,512]{1,0:T(8,128)(2,1)S(1)} collective-permute-done((bf16[256,512]{1,0:T(8,128)(2,1)S(1)}, bf16[256,512]{1,0:T(8,128)(2,1)S(1)}, u32[]{:S(2)}, u32[]{:S(2)}) %collective-permute-start.3) | collective-permute-done | bytes 262176 | tf_op jit(solution)/shard_map/ppermute | solution.py:16
  259.7 3.1 fusion.16
  268.7 3.1 fusion.10
  277.5 3.1 fusion.13
  292.8 6.0 %collective-permute-start.8 = (bf16[256,512]{0,1:T(8,128)(2,1)}, bf16[256,512]{0,1:T(8,128)(2,1)}, u32[]{:S(2)}, u32[]{:S(2)}) collective-permute-start(bf16[256,512]{0,1:T(8,128)(2,1)} %get-tuple-element.40), channel_id=1, source_target_pairs={{24,0},{32,8},{40,16},{48,24},{56,32},{64,40},{72,48},{80,56},{88,... | collective-permute-start | bytes 786440 | tf_op jit(solution)/shard_map/ppermute | solution.py:16
  304.6 6.0 %all-to-all-start.1 = ((f32[8,16,512]{2,1,0:T(8,128)}), f32[8,16,512]{2,1,0:T(8,128)S(1)}, u32[]{:S(2)}, u32[]{:S(2)}) async-start(f32[8,16,512]{2,1,0:T(8,128)} %bitcast.79), calls=%async_computation.1 | async-start | bytes 524288 | tf_op jit(solution)/shard_map/all_to_all | solution.py:32
  313.4 11.0 %collective-permute-done.7 = bf16[256,512]{0,1:T(8,128)(2,1)} collective-permute-done((bf16[256,512]{0,1:T(8,128)(2,1)}, bf16[256,512]{0,1:T(8,128)(2,1)}, u32[]{:S(2)}, u32[]{:S(2)}) %collective-permute-start.7) | collective-permute-done | bytes 262176 | tf_op jit(solution)/shard_map/ppermute | solution.py:16
  (156 shorter events, 89.7 us)
Async XLA Ops:
  7.2 109.3 %copy-start = (bf16[1,256,4096]{2,1,0:T(8,128)(2,1)S(1)}, bf16[1,256,4096]{2,1,0:T(8,128)(2,1)}, u32[]{:S(2)}) copy-start(bf16[1,256,4096]{2,1,0:T(8,128)(2,1)} %param.7) | copy-start | bytes 6291460
  7.2 123.0 %all-gather.2.cloned.1.call-start = ((), (), s32[]{:S(2)}) async-start(), calls=%async_computation.2 | async-start | bytes 4718592 | tf_op jit(solution)/shard_map/all_gather | solution.py:124
  7.2 30.1 %collective-permute-start.2 = (bf16[256,512]{1,0:T(8,128)(2,1)}, bf16[256,512]{1,0:T(8,128)(2,1)}, u32[]{:S(2)}, u32[]{:S(2)}) collective-permute-start(bf16[256,512]{1,0:T(8,128)(2,1)} %bitcast.328), channel_id=1, source_target_pairs={{0,8},{8,16},{16,24},{24,32},{32,40},{40,48},{48,56},{56,64},{64,7... | collective-permute-start | bytes 786440 | tf_op jit(solution)/shard_map/ppermute | solution.py:16
  9.3 28.1 %collective-permute-start.1 = (bf16[256,512]{1,0:T(8,128)(2,1)}, bf16[256,512]{1,0:T(8,128)(2,1)}, u32[]{:S(2)}, u32[]{:S(2)}) collective-permute-start(bf16[256,512]{1,0:T(8,128)(2,1)} %bitcast.329), channel_id=1, source_target_pairs={{0,16},{8,24},{16,32},{24,40},{32,48},{40,56},{48,64},{56,72},{64,... | collective-permute-start | bytes 786440 | tf_op jit(solution)/shard_map/ppermute | solution.py:16
  14.5 33.3 %collective-permute-start = (bf16[256,512]{1,0:T(8,128)(2,1)}, bf16[256,512]{1,0:T(8,128)(2,1)}, u32[]{:S(2)}, u32[]{:S(2)}) collective-permute-start(bf16[256,512]{1,0:T(8,128)(2,1)} %bitcast.330), channel_id=1, source_target_pairs={{0,24},{8,32},{16,40},{24,48},{32,56},{40,64},{48,72},{56,80},{64,... | collective-permute-start | bytes 786440 | tf_op jit(solution)/shard_map/ppermute | solution.py:16
  34.9 12.9 %copy-start.39 = (bf16[1,256,512]{2,1,0:T(8,128)(2,1)S(1)}, bf16[1,256,512]{2,1,0:T(8,128)(2,1)}, u32[]{:S(2)}) copy-start(bf16[1,256,512]{2,1,0:T(8,128)(2,1)} %param.9) | copy-start | bytes 786436
  86.9 22.4 %collective-permute-start.9 = (bf16[256,512]{0,1:T(8,128)(2,1)S(1)}, bf16[256,512]{0,1:T(8,128)(2,1)S(1)}, u32[]{:S(2)}, u32[]{:S(2)}) collective-permute-start(bf16[256,512]{0,1:T(8,128)(2,1)S(1)} %get-tuple-element.36), channel_id=1, source_target_pairs={{8,0},{16,8},{24,16},{32,24},{40,32},{48,40},{56,48},{64,56},{72,6... | collective-permute-start | bytes 786440 | tf_op jit(solution)/shard_map/ppermute | solution.py:16
  88.8 23.3 %collective-permute-start.11 = (bf16[256,512]{0,1:T(8,128)(2,1)S(1)}, bf16[256,512]{0,1:T(8,128)(2,1)S(1)}, u32[]{:S(2)}, u32[]{:S(2)}) collective-permute-start(bf16[256,512]{0,1:T(8,128)(2,1)S(1)} %get-tuple-element.37), channel_id=1, source_target_pairs={{24,0},{32,8},{40,16},{48,24},{56,32},{64,40},{72,48},{80,56},{88,... | collective-permute-start | bytes 786440 | tf_op jit(solution)/shard_map/ppermute | solution.py:16
  94.2 22.2 %collective-permute-start.10 = (bf16[256,512]{0,1:T(8,128)(2,1)S(1)}, bf16[256,512]{0,1:T(8,128)(2,1)S(1)}, u32[]{:S(2)}, u32[]{:S(2)}) collective-permute-start(bf16[256,512]{0,1:T(8,128)(2,1)S(1)} %get-tuple-element.38), channel_id=1, source_target_pairs={{16,0},{24,8},{32,16},{40,24},{48,32},{56,40},{64,48},{72,56},{80,... | collective-permute-start | bytes 786440 | tf_op jit(solution)/shard_map/ppermute | solution.py:16
  121.0 180.0 %all-to-all-start = ((bf16[32,128,512]{1,2,0:T(8,128)(2,1)}), bf16[32,128,512]{1,2,0:T(8,128)(2,1)}, u32[]{:S(2)}, u32[]{:S(2)}) async-start(bf16[32,128,512]{1,2,0:T(8,128)(2,1)} %bitcast.302), calls=%async_computation | async-start | bytes 8388608 | tf_op jit(solution)/shard_map/all_to_all | solution.py:26
  130.2 15.3 %copy-start.24 = (bf16[4096,512]{1,0:T(8,128)(2,1)S(1)}, bf16[4096,512]{1,0:T(8,128)(2,1)}, u32[]{:S(2)}) copy-start(bf16[4096,512]{1,0:T(8,128)(2,1)} %all-gather.2.cloned.1.call-done) | copy-start | bytes 12582916
  133.8 106.6 %collective-permute-start.5 = (bf16[256,512]{1,0:T(8,128)(2,1)S(1)}, bf16[256,512]{1,0:T(8,128)(2,1)S(1)}, u32[]{:S(2)}, u32[]{:S(2)}) collective-permute-start(bf16[256,512]{1,0:T(8,128)(2,1)S(1)} %fusion.45), channel_id=1, source_target_pairs={{0,8},{8,16},{16,24},{24,32},{32,40},{40,48},{48,56},{56,64},{64,7... | collective-permute-start | bytes 786440 | tf_op jit(solution)/shard_map/ppermute | solution.py:16
  135.8 105.5 %collective-permute-start.4 = (bf16[256,512]{1,0:T(8,128)(2,1)S(1)}, bf16[256,512]{1,0:T(8,128)(2,1)S(1)}, u32[]{:S(2)}, u32[]{:S(2)}) collective-permute-start(bf16[256,512]{1,0:T(8,128)(2,1)S(1)} %fusion.45), channel_id=1, source_target_pairs={{0,16},{8,24},{16,32},{24,40},{32,48},{40,56},{48,64},{56,72},{64,... | collective-permute-start | bytes 786440 | tf_op jit(solution)/shard_map/ppermute | solution.py:16
  140.1 112.2 %collective-permute-start.3 = (bf16[256,512]{1,0:T(8,128)(2,1)S(1)}, bf16[256,512]{1,0:T(8,128)(2,1)S(1)}, u32[]{:S(2)}, u32[]{:S(2)}) collective-permute-start(bf16[256,512]{1,0:T(8,128)(2,1)S(1)} %fusion.45), channel_id=1, source_target_pairs={{0,24},{8,32},{16,40},{24,48},{32,56},{40,64},{48,72},{56,80},{64,... | collective-permute-start | bytes 786440 | tf_op jit(solution)/shard_map/ppermute | solution.py:16
  145.5 106.9 %copy-start.31 = (bf16[256,512]{0,1:T(8,128)(2,1)S(1)}, bf16[256,512]{0,1:T(8,128)(2,1)}, u32[]{:S(2)}) copy-start(bf16[256,512]{0,1:T(8,128)(2,1)} %get-tuple-element.47) | copy-start | bytes 786436
  145.5 107.4 %copy-start.25 = (f32[4,256,1024]{1,2,0:T(8,128)S(1)}, f32[4,256,1024]{1,2,0:T(8,128)}, u32[]{:S(2)}) copy-start(f32[4,256,1024]{1,2,0:T(8,128)} %get-tuple-element.51) | copy-start | bytes 12582916
  148.1 104.3 %copy-start.9 = (bf16[4,256,1024]{1,2,0:T(8,128)(2,1)S(1)}, bf16[4,256,1024]{1,2,0:T(8,128)(2,1)}, u32[]{:S(2)}) copy-start(bf16[4,256,1024]{1,2,0:T(8,128)(2,1)} %copy-done.8) | copy-start | bytes 6291460
  290.9 22.4 %collective-permute-start.6 = (bf16[256,512]{0,1:T(8,128)(2,1)}, bf16[256,512]{0,1:T(8,128)(2,1)}, u32[]{:S(2)}, u32[]{:S(2)}) collective-permute-start(bf16[256,512]{0,1:T(8,128)(2,1)} %get-tuple-element.39), channel_id=1, source_target_pairs={{8,0},{16,8},{24,16},{32,24},{40,32},{48,40},{56,48},{64,56},{72,6... | collective-permute-start | bytes 786440 | tf_op jit(solution)/shard_map/ppermute | solution.py:16
  292.8 20.5 %collective-permute-start.8 = (bf16[256,512]{0,1:T(8,128)(2,1)}, bf16[256,512]{0,1:T(8,128)(2,1)}, u32[]{:S(2)}, u32[]{:S(2)}) collective-permute-start(bf16[256,512]{0,1:T(8,128)(2,1)} %get-tuple-element.40), channel_id=1, source_target_pairs={{24,0},{32,8},{40,16},{48,24},{56,32},{64,40},{72,48},{80,56},{88,... | collective-permute-start | bytes 786440 | tf_op jit(solution)/shard_map/ppermute | solution.py:16
  298.8 11.8 %copy-start.32 = (bf16[256,512]{1,0:T(8,128)(2,1)S(1)}, bf16[256,512]{1,0:T(8,128)(2,1)}, u32[]{:S(2)}) copy-start(bf16[256,512]{1,0:T(8,128)(2,1)} %copy.188) | copy-start | bytes 786436
  298.9 11.8 %copy-start.33 = (bf16[256,512]{1,0:T(8,128)(2,1)S(1)}, bf16[256,512]{1,0:T(8,128)(2,1)}, u32[]{:S(2)}) copy-start(bf16[256,512]{1,0:T(8,128)(2,1)} %copy.185) | copy-start | bytes 786436
  298.9 25.4 %collective-permute-start.7 = (bf16[256,512]{0,1:T(8,128)(2,1)}, bf16[256,512]{0,1:T(8,128)(2,1)}, u32[]{:S(2)}, u32[]{:S(2)}) collective-permute-start(bf16[256,512]{0,1:T(8,128)(2,1)} %get-tuple-element.41), channel_id=1, source_target_pairs={{16,0},{24,8},{32,16},{40,24},{48,32},{56,40},{64,48},{72,56},{80,... | collective-permute-start | bytes 786440 | tf_op jit(solution)/shard_map/ppermute | solution.py:16
  304.6 24.4 %all-to-all-start.1 = ((f32[8,16,512]{2,1,0:T(8,128)}), f32[8,16,512]{2,1,0:T(8,128)S(1)}, u32[]{:S(2)}, u32[]{:S(2)}) async-start(f32[8,16,512]{2,1,0:T(8,128)} %bitcast.79), calls=%async_computation.1 | async-start | bytes 524288 | tf_op jit(solution)/shard_map/all_to_all | solution.py:32
  311.8 17.9 %copy-start.1 = (bf16[1,256,4096]{2,1,0:T(8,128)(2,1)S(1)}, bf16[1,256,4096]{2,1,0:T(8,128)(2,1)}, u32[]{:S(2)}) copy-start(bf16[1,256,4096]{2,1,0:T(8,128)(2,1)} %param.7) | copy-start | bytes 6291460
  (31 other events, 83.1 us)
Sparse Core Ops, SparseCore 0:
  21.9 59.6 all-gather.1
where the time goes:
time: 338 us; the launch traced here: 337 us
  waiting for transfers between devices  145 us (43%)
  starting transfers between devices  63.6 us (19%)
  matrix products  54.5 us (16%)
  local copies, waits for them, and re-layouts  28.2 us (8%)
  other arithmetic  25 us (7%)
  between operations  19.9 us (6%)
    ppermute x12, waiting for transfers between devices, from_behind(): return lax.ppermute(block, axis, route)  143 us
    ppermute x12, starting transfers between devices, from_behind(): return lax.ppermute(block, axis, route)  48.3 us
    sub x4, matrix products, window_grads(): expd = jnp.exp(scores - peak)  18.6 us
    unnamed x83, local copies, waits for them, and re-layouts  14.9 us
    convert_element_type x4, other arithmetic, window_grads(): attn_low = attn_probs.astype(jnp.bfloat16)  10.4 us
    dot_general x4, matrix products, window_grads(): jnp.einsum('tjd,wd->jtw', g_cols, v_cols, preferred_element_type=jnp.floa...  9.98 us
    all_to_all x1, starting transfers between devices, sent_and_summed(): lax.all_to_all(pieces, axis, split_axis=0, concat_axis=0, tiled=True)  9.19 us
  transfers between devices with their start and end apart: 15, of which 9 were waited for; matrix products, arithmetic and copies ran while one was open for 29% of the time, Pallas kernels for 0%

commit v1 on v0

v1 whole, which is shorter than its diff:
```python
import functools

import jax
import jax.numpy as jnp
from jax import lax
from jax.experimental import pallas as pl
from jax.experimental.pallas import tpu as pltpu
from jax.sharding import Mesh, PartitionSpec as P

HD = 128
GROUP = 4
KVH = 4
BLK = 256
DOCB = 4
SCALE = HD**-0.5
EXP2_SCALE = SCALE * 1.4426950408889634
BF = jnp.bfloat16
F32 = jnp.float32

NODE = ("x", "h", "c")
LOCAL = ("l", "y")


def dot(a, b, ca, cb):
    return lax.dot_general(a, b, (((ca,), (cb,)), ((), ())), preferred_element_type=F32)


def node_shift(block, pairs):
    return lax.ppermute(block, NODE, pairs)


def core_swap(block):
    return lax.ppermute(block, "c", [(0, 1), (1, 0)])


def window_in(block, nodes):
    behind2 = node_shift(block, [(i, i + 2) for i in range(nodes - 2)])
    behind3 = node_shift(behind2, [(i, i + 1) for i in range(1, nodes - 1, 2)])
    swapped = core_swap(jnp.stack([block, behind2]))
    return behind2, behind3, swapped


def window_out(own, two, sent, core, nodes):
    swapped = core_swap(sent)
    first = core == 0
    own = own + jnp.where(first, swapped[0], jnp.zeros_like(swapped[0])).astype(F32)
    two = two + jnp.where(first, swapped[1], swapped[0]).astype(F32)
    passed = node_shift(swapped[1], [(i, i - 2) for i in range(3, nodes, 2)])
    two = (two + passed.astype(F32)).astype(BF)
    got = node_shift(two, [(i, i - 2) for i in range(2, nodes)])
    return (own + got.astype(F32)).astype(BF)


def find_doc(node, lens_ref, order_ref):
    slots = lens_ref.shape[1]

    def step(j, carry):
        start, doc_start, length = carry
        own = lens_ref[0, order_ref[0, j]]
        count = (own + (BLK - 1)) >> 8
        inside = (start <= node) & (node < start + count)
        doc_start = jnp.where(inside, start, doc_start)
        length = jnp.where(inside, own, length)
        return start + count, doc_start, length

    zero = jnp.int32(0)
    _, doc_start, length = lax.fori_loop(0, slots, step, (zero, zero, zero))
    before = node - doc_start
    return before, length - before * BLK


def fill_window(core, own, two, three, swapped, win):
    win[0:BLK] = own[...]
    win[2 * BLK : 3 * BLK] = two[...]

    @pl.when(core == 0)
    def _():
        win[BLK : 2 * BLK] = swapped[1]
        win[3 * BLK : 4 * BLK] = three[...]

    @pl.when(core != 0)
    def _():
        win[BLK : 2 * BLK] = swapped[0]
        win[3 * BLK : 4 * BLK] = swapped[1]


def stack_heads(src, dst, mask=None):
    for j in range(GROUP):
        cols = src[:, j * HD : (j + 1) * HD]
        dst[j * BLK : (j + 1) * BLK] = cols if mask is None else cols * mask


def row_mask(real):
    rows = lax.broadcasted_iota(jnp.int32, (BLK, HD), 0)
    return jnp.where(rows < real, 1.0, 0.0).astype(BF)


def probs_kernel(
    where_ref, lens_ref, order_ref, q_ref, g_ref, k0, k2, k3, ks,
    p_ref, dv0_ref, dv2_ref, dvs_ref, kwin, qst, gst, info,
):
    core = where_ref[1]

    @pl.when(pl.program_id(0) == 0)
    def _():
        before, real = find_doc(where_ref[0], lens_ref, order_ref)
        info[0] = before
        info[1] = real

    before = info[0]
    fill_window(core, k0, k2, k3, ks, kwin)
    stack_heads(q_ref, qst)
    stack_heads(g_ref, gst, row_mask(info[1]))
    key_id = lax.broadcasted_iota(jnp.int32, (BLK, BLK), 0)
    query_id = lax.broadcasted_iota(jnp.int32, (BLK, BLK), 1)
    causal = key_id <= query_id
    for j in range(GROUP):
        qj = qst[j * BLK : (j + 1) * BLK]
        scores = [dot(kwin[w * BLK : (w + 1) * BLK], qj, 1, 1) for w in range(DOCB)]
        scores[0] = jnp.where(causal, scores[0], -1e30)
        peaks = [jnp.max(s, axis=0, keepdims=True) for s in scores]
        peak = peaks[0]
        for w in range(1, DOCB):
            peak = jnp.maximum(peak, jnp.where(before >= w, peaks[w], -1e30))
        total = jnp.zeros((1, BLK), F32)
        expd = []
        for w in range(DOCB):
            base = peak if w == 0 else jnp.where(before >= w, peak, 1e30)
            e = jnp.exp2((scores[w] - base) * EXP2_SCALE)
            total = total + jnp.sum(e, axis=0, keepdims=True)
            expd.append(e)
        inv = 1.0 / total
        for w in range(DOCB):
            p_ref[0, w * BLK : (w + 1) * BLK, j * BLK : (j + 1) * BLK] = (expd[w] * inv).astype(BF)
    terms = [dot(p_ref[0, w * BLK : (w + 1) * BLK, :], gst[...], 1, 0) for w in range(DOCB)]
    dv0_ref[...] = terms[0]
    dv2_ref[...] = terms[2]
    dvs_ref[0] = terms[1].astype(BF)
    dvs_ref[1] = terms[3].astype(BF)


def grads_kernel(
    where_ref, lens_ref, order_ref, q_ref, g_ref, k0, k2, k3, ks, v0, v2, v3, vs, p_ref,
    dq_ref, dk0_ref, dk2_ref, dks_ref, kwin, vwin, qst, gst, dst, info,
):
    core = where_ref[1]

    @pl.when(pl.program_id(0) == 0)
    def _():
        _, real = find_doc(where_ref[0], lens_ref, order_ref)
        info[0] = real

    fill_window(core, k0, k2, k3, ks, kwin)
    fill_window(core, v0, v2, v3, vs, vwin)
    stack_heads(q_ref, qst)
    stack_heads(g_ref, gst, row_mask(info[0]))
    key_t = jnp.transpose(kwin[...])
    for j in range(GROUP):
        gj = gst[j * BLK : (j + 1) * BLK]
        delta = jnp.zeros((1, BLK), F32)
        grads = []
        for w in range(DOCB):
            pg = dot(vwin[w * BLK : (w + 1) * BLK], gj, 1, 1)
            p = p_ref[0, w * BLK : (w + 1) * BLK, j * BLK : (j + 1) * BLK].astype(F32)
            delta = delta + jnp.sum(p * pg, axis=0, keepdims=True)
            grads.append(pg)
        for w in range(DOCB):
            p = p_ref[0, w * BLK : (w + 1) * BLK, j * BLK : (j + 1) * BLK].astype(F32)
            dst[w * BLK : (w + 1) * BLK, j * BLK : (j + 1) * BLK] = (p * (grads[w] - delta)).astype(BF)
        dq_t = dot(key_t, dst[:, j * BLK : (j + 1) * BLK], 1, 0) * SCALE
        dq_ref[:, j * HD : (j + 1) * HD] = jnp.transpose(dq_t).astype(BF)
    terms = [dot(dst[w * BLK : (w + 1) * BLK, :], qst[...], 1, 0) * SCALE for w in range(DOCB)]
    dk0_ref[...] = terms[0]
    dk2_ref[...] = terms[2]
    dks_ref[0] = terms[1].astype(BF)
    dks_ref[1] = terms[3].astype(BF)


SMEM = pl.BlockSpec(memory_space=pltpu.SMEM)
HEADS = pl.BlockSpec((BLK, GROUP * HD), lambda g: (0, g))
ONE = pl.BlockSpec((BLK, HD), lambda g: (0, g))
PAIR = pl.BlockSpec((2, BLK, HD), lambda g: (0, 0, g))
PROBS = pl.BlockSpec((1, DOCB * BLK, GROUP * BLK), lambda g: (g, 0, 0))
KVW = KVH * HD
TERMS = (
    jax.ShapeDtypeStruct((BLK, KVW), F32),
    jax.ShapeDtypeStruct((BLK, KVW), F32),
    jax.ShapeDtypeStruct((2, BLK, KVW), BF),
)


def run_probs(where, lens, order, q, g, k0, k2, k3, ks):
    return pl.pallas_call(
        probs_kernel,
        grid=(KVH,),
        in_specs=[SMEM, SMEM, SMEM, HEADS, HEADS, ONE, ONE, ONE, PAIR],
        out_specs=(PROBS, ONE, ONE, PAIR),
        out_shape=(jax.ShapeDtypeStruct((KVH, DOCB * BLK, GROUP * BLK), BF),) + TERMS,
        scratch_shapes=[
            pltpu.VMEM((DOCB * BLK, HD), BF),
            pltpu.VMEM((GROUP * BLK, HD), BF),
            pltpu.VMEM((GROUP * BLK, HD), BF),
            pltpu.SMEM((2,), jnp.int32),
        ],
        name="probs",
    )(where, lens, order, q, g, k0, k2, k3, ks)


def run_grads(where, lens, order, q, g, k0, k2, k3, ks, v0, v2, v3, vs, probs):
    return pl.pallas_call(
        grads_kernel,
        grid=(KVH,),
        in_specs=[SMEM, SMEM, SMEM, HEADS, HEADS] + [ONE, ONE, ONE, PAIR] * 2 + [PROBS],
        out_specs=(HEADS, ONE, ONE, PAIR),
        out_shape=(jax.ShapeDtypeStruct(q.shape, BF),) + TERMS,
        scratch_shapes=[
            pltpu.VMEM((DOCB * BLK, HD), BF),
            pltpu.VMEM((DOCB * BLK, HD), BF),
            pltpu.VMEM((GROUP * BLK, HD), BF),
            pltpu.VMEM((GROUP * BLK, HD), BF),
            pltpu.VMEM((DOCB * BLK, GROUP * BLK), BF),
            pltpu.SMEM((1,), jnp.int32),
        ],
        name="grads",
    )(where, lens, order, q, g, k0, k2, k3, ks, v0, v2, v3, vs, probs)


def split_kernel(where_ref, x_ref, keep_ref, send_ref):
    even = jnp.transpose(x_ref[:, :HD])
    odd = jnp.transpose(x_ref[:, HD:])

    @pl.when(where_ref[1] == 0)
    def _():
        keep_ref[...] = even
        send_ref[...] = odd

    @pl.when(where_ref[1] != 0)
    def _():
        keep_ref[...] = odd
        send_ref[...] = even


def split_columns(where, x):
    rows, width = x.shape
    half = jax.ShapeDtypeStruct((width // 2, rows), BF)
    out = pl.BlockSpec((HD, rows), lambda i: (i, 0))
    return pl.pallas_call(
        split_kernel,
        grid=(width // (2 * HD),),
        in_specs=[SMEM, pl.BlockSpec((rows, 2 * HD), lambda i: (0, i))],
        out_specs=(out, out),
        out_shape=(half, half),
        name="split",
    )(where, x)


def values_kernel(where_ref, x_ref, wa_ref, wb_ref, out_ref, acc_a, acc_b):
    step = pl.program_id(0)

    @pl.when(step == 0)
    def _():
        acc_a[...] = jnp.zeros_like(acc_a)
        acc_b[...] = jnp.zeros_like(acc_b)

    acc_a[...] += dot(x_ref[...], wa_ref[...], 1, 0)
    acc_b[...] += dot(x_ref[...], wb_ref[...], 1, 0)
    half = acc_a.shape[1]

    @pl.when(step == pl.num_programs(0) - 1)
    def _():
        a, b = acc_a[...].astype(BF), acc_b[...].astype(BF)

        @pl.when(where_ref[1] == 0)
        def _():
            out_ref[:, :half] = a
            out_ref[:, half:] = b

        @pl.when(where_ref[1] != 0)
        def _():
            out_ref[:, :half] = b
            out_ref[:, half:] = a


def run_values(where, x, wa, wb):
    rows, width = x.shape
    half = wa.shape[1]
    piece = 1024
    weight = pl.BlockSpec((piece, half), lambda i: (i, 0))
    return pl.pallas_call(
        values_kernel,
        grid=(width // piece,),
        in_specs=[SMEM, pl.BlockSpec((rows, piece), lambda i: (0, i)), weight, weight],
        out_specs=pl.BlockSpec((rows, 2 * half), lambda i: (0, 0)),
        out_shape=jax.ShapeDtypeStruct((rows, 2 * half), BF),
        scratch_shapes=[pltpu.VMEM((rows, half), F32), pltpu.VMEM((rows, half), F32)],
        name="values",
    )(where, x, wa, wb)


def input_grad_kernel(where_ref, v_ref, wa_ref, wb_ref, out_ref, va, vb):
    half = va.shape[1]

    @pl.when(pl.program_id(0) == 0)
    def _():
        @pl.when(where_ref[1] == 0)
        def _():
            va[...] = v_ref[:, :half]
            vb[...] = v_ref[:, half:]

        @pl.when(where_ref[1] != 0)
        def _():
            va[...] = v_ref[:, half:]
            vb[...] = v_ref[:, :half]

    out = dot(va[...], wa_ref[...], 1, 1) + dot(vb[...], wb_ref[...], 1, 1)
    out_ref[...] = out.astype(BF)


def run_input_grad(where, v, wa, wb):
    rows = v.shape[0]
    width, half = wa.shape
    piece = 1024
    weight = pl.BlockSpec((piece, half), lambda i: (i, 0))
    return pl.pallas_call(
        input_grad_kernel,
        grid=(width // piece,),
        in_specs=[SMEM, pl.BlockSpec(v.shape, lambda i: (0, 0)), weight, weight],
        out_specs=pl.BlockSpec((rows, piece), lambda i: (0, i)),
        out_shape=jax.ShapeDtypeStruct((rows, width), BF),
        scratch_shapes=[pltpu.VMEM((rows, half), BF), pltpu.VMEM((rows, half), BF)],
        name="input_grad",
    )(where, v, wa, wb)


def weight_grad_kernel(xa_ref, xb_ref, va_ref, vb_ref, out_ref):
    part = dot(xa_ref[...], va_ref[...], 1, 0) + dot(xb_ref[...], vb_ref[...], 1, 0)
    part = part.astype(BF)
    for h in range(4):
        for l in range(2):
            for y in range(4):
                row = ((h * 2 + l) * 4 + y) * 16
                out_ref[0, y, h * 2 + l] = part[row : row + 16]


def run_weight_grad(xa, xb, va, vb):
    rows, tokens = xa.shape
    width = va.shape[1]
    piece = rows // 4
    x_spec = pl.BlockSpec((piece, tokens), lambda i: (i, 0))
    v_spec = pl.BlockSpec(va.shape, lambda i: (0, 0))
    return pl.pallas_call(
        weight_grad_kernel,
        grid=(4,),
        in_specs=[x_spec, x_spec, v_spec, v_spec],
        out_specs=pl.BlockSpec((1, 4, 8, 16, width), lambda i: (i, 0, 0, 0, 0)),
        out_shape=jax.ShapeDtypeStruct((4, 4, 8, 16, width), BF),
        name="weight_grad",
    )(xa, xb, va, vb)


def exchanged(pieces, axes):
    return lax.all_to_all(pieces, axes, split_axis=0, concat_axis=0, tiled=True)


def local(hidden, queries, saved_keys, grad_out, value_weight, lens, order):
    node = lax.axis_index(NODE).astype(jnp.int32)
    core = lax.axis_index("c").astype(jnp.int32)
    nodes = lax.axis_size(NODE)
    where = jnp.stack([node, core])
    x, q, k, g = hidden[0], queries[0], saved_keys[0], grad_out[0]

    k2, k3, ks = window_in(k, nodes)

    half = value_weight.shape[1] // 2
    mine = lax.dynamic_slice_in_dim(value_weight, core * half, half, 1)
    group = lax.axis_size(LOCAL)
    weight_a = exchanged(jnp.broadcast_to(mine[None], (group,) + mine.shape), LOCAL)
    weight_a = weight_a.reshape(-1, half)
    weight_b = core_swap(weight_a)

    kept, sent = split_columns(where, x)
    brought = core_swap(sent)

    probs, dv0, dv2, dvs = run_probs(where, lens, order, q, g, k, k2, k3, ks)
    values = run_values(where, x, weight_a, weight_b)
    v2, v3, vs = window_in(values, nodes)
    value_low = window_out(dv0, dv2, dvs, core, nodes)

    part = run_weight_grad(kept, brought, value_low, core_swap(value_low))
    part = exchanged(part.reshape(16, 128, -1), ("x", "y"))
    part = part.astype(F32).sum(axis=0).astype(BF)
    part = exchanged(part.reshape(8, 16, -1), ("h", "l"))
    weight_grad = part.astype(F32).sum(axis=0)

    query_grad, dk0, dk2, dks = run_grads(
        where, lens, order, q, g, k, k2, k3, ks, values, v2, v3, vs, probs
    )
    key_grad = window_out(dk0, dk2, dks, core, nodes)
    input_grad = run_input_grad(where, value_low, weight_a, weight_b)
    return query_grad[None], key_grad[None], input_grad[None], weight_grad


def solution(mesh):
    parts = Mesh(mesh.devices.reshape(4, 4, 2, 2, 4), ("x", "h", "c", "l", "y"))
    rows = P(LOCAL, NODE, None)
    return jax.shard_map(
        local,
        mesh=parts,
        in_specs=(rows, rows, rows, rows, P(LOCAL, None), P(LOCAL, None), P(LOCAL, None)),
        out_specs=(rows, rows, rows, P(NODE + LOCAL, None)),
        check_vma=False,
    )
```

time: 338 us -> 197 us (0.58)
  waiting for transfers between devices: 145 us -> 86.6 us
  matrix products: 54.5 us -> 0 us
  Pallas kernels: 0 us -> 52.1 us
  local copies, waits for them, and re-layouts: 28.2 us -> 4.94 us
  starting transfers between devices: 63.6 us -> 41.8 us
  between operations: 19.9 us -> 0.88 us
  other arithmetic: 25 us -> 9.16 us
    ppermute x12 -> x15, waiting for transfers between devices: 143 us -> 81.7 us  [the longest x8 75.9 us: node_shift(): return lax.ppermute(block, NODE, pairs)]
    pallas_call x0 -> x6, Pallas kernels: none -> 52.1 us  [the longest x1 14.6 us: run_grads(): pl.pallas_call(grads_kernel, grid=(KVH,), in_specs=[SMEM, SMEM, SMEM, HEA...]
    dot_general x23 -> x0, matrix products: 35.9 us -> none  [the longest x4 9.98 us: window_grads(): jnp.einsum('tjd,wd->jtw', g_cols, v_cols, preferred_element_type=jnp.floa...]
    ppermute x12 -> x15, starting transfers between devices: 48.3 us -> 24.3 us  [the longest x8 22 us: node_shift(): return lax.ppermute(block, NODE, pairs)]
    sub x4 -> x0, matrix products: 18.6 us -> none  [window_grads(): expd = jnp.exp(scores - peak)]
    unnamed x83 -> x24, local copies, waits for them, and re-layouts: 14.9 us -> 3.43 us
    reshape x5 -> x0, local copies, waits for them, and re-layouts: 9.43 us -> none  [the longest x4 6.25 us: window_grads(): head_query.astype(jnp.bfloat16).reshape(row_count, group * HD)]
    convert_element_type x6 -> x3, other arithmetic: 11.1 us -> 2.57 us  [the longest x2 1.4 us: window_out(): two = (two + passed.astype(F32)).astype(BF)]
  transfers between devices with their start and end apart: 15 -> 18, of which waited for: 9 -> 10; matrix products, arithmetic and copies ran while one was open for 29% -> 4% of each run, Pallas kernels for 0% -> 27%
where the time goes in v1:
time: 197 us; the launch traced here: 195 us
  waiting for transfers between devices  86.6 us (44%)
  Pallas kernels  52.1 us (26%)
  starting transfers between devices  41.8 us (21%)
  other arithmetic  9.16 us (5%)
  local copies, waits for them, and re-layouts  4.94 us (3%)
    ppermute x8, waiting for transfers between devices, node_shift(): return lax.ppermute(block, NODE, pairs)  75.9 us
    ppermute x8, starting transfers between devices, node_shift(): return lax.ppermute(block, NODE, pairs)  22 us
    all_to_all x3, starting transfers between devices, exchanged(): return lax.all_to_all(pieces, axes, split_axis=0, concat_axis=0, tiled=True)  17.5 us
    pallas_call x1, Pallas kernels, run_grads(): pl.pallas_call(grads_kernel, grid=(KVH,), in_specs=[SMEM, SMEM, SMEM, HEA...  14.6 us
    pallas_call x1, Pallas kernels, run_probs(): pl.pallas_call(probs_kernel, grid=(KVH,), in_specs=[SMEM, SMEM, SMEM, HEA...  12.5 us
    pallas_call x1, Pallas kernels, split_columns(): pl.pallas_call(split_kernel, grid=(width // (2 * HD),), in_specs=[SMEM, p...  9.97 us
    ppermute x7, waiting for transfers between devices, core_swap(): return lax.ppermute(block, 'c', [(0, 1), (1, 0)])  5.74 us
    pallas_call x1, Pallas kernels, run_input_grad(): pl.pallas_call(input_grad_kernel, grid=(width // piece,), in_specs=[SMEM,...  5.18 us
  transfers between devices with their start and end apart: 18, of which 10 were waited for; matrix products, arithmetic and copies ran while one was open for 4% of the time, Pallas kernels for 27%

profile of v1, /device:TPU:2, one launch (start us, length us, event | category | flops | bytes accessed | tf_op | source)
XLA Modules:
  0.0 195.4 jit_solution(11037806174308490736)
XLA Ops:
  3.2 6.0 %all-to-all-start = ((bf16[8,512,256]{2,1,0:T(8,128)(2,1)}), bf16[8,512,256]{2,1,0:T(8,128)(2,1)S(1)}, u32[]{:S(2)}, u32[]{:S(2)}) async-start(bf16[8,512,256]{2,1,0:T(8,128)(2,1)} %broadcast_in_dim.15), calls=%async_computation | async-start | bytes 4194304 | tf_op jit(solution)/shard_map/all_to_all | solution.py:362
  9.1 5.2 %collective-permute-start = (bf16[256,512]{1,0:T(8,128)(2,1)S(1)}, bf16[256,512]{1,0:T(8,128)(2,1)S(1)}, u32[]{:S(2)}, u32[]{:S(2)}) collective-permute-start(bf16[256,512]{1,0:T(8,128)(2,1)S(1)} %bitcast.48), channel_id=1, source_target_pairs={{0,16},{8,24},{16,32},{24,40},{32,48},{40,56},{48,64},{56,72},{64,... | collective-permute-start | bytes 786440 | tf_op jit(solution)/shard_map/ppermute | solution.py:29
  14.3 37.4 %collective-permute-done.k2 = bf16[256,512]{1,0:T(8,128)(2,1)S(1)} collective-permute-done((bf16[256,512]{1,0:T(8,128)(2,1)S(1)}, bf16[256,512]{1,0:T(8,128)(2,1)S(1)}, u32[]{:S(2)}, u32[]{:S(2)}) %collective-permute-start) | collective-permute-done | bytes 262176 | tf_op jit(solution)/shard_map/ppermute | solution.py:29
  55.7 7.7 %collective-permute-done.1.k3 = bf16[256,512]{1,0:T(8,128)(2,1)} collective-permute-done((bf16[256,512]{1,0:T(8,128)(2,1)S(1)}, bf16[256,512]{1,0:T(8,128)(2,1)}, u32[]{:S(2)}, u32[]{:S(2)}) %collective-permute-start.1) | collective-permute-done | bytes 262176 | tf_op jit(solution)/shard_map/ppermute | solution.py:29
  64.2 12.5 %probs.1 = (bf16[4,1024,1024]{2,1,0:T(8,128)(2,1)}, f32[256,512]{1,0:T(8,128)}, f32[256,512]{1,0:T(8,128)}, bf16[2,256,512]{2,1,0:T(8,128)(2,1)}) custom-call(s32[2]{0:T(128)} %pad_add_fusion.where_ref, s32[1,32]{1,0:T(1,128)} %lens_ref.3, s32[1,32]{1,0:T(1,128)} %order_ref.3, bf16[256,2048]{1,0:T(8,128)(2,1)} %bitcast.42, bf16[256,2048]{1,0:T(8,128)(2,1)} %bitcast.44, ...), custom_call_target="tpu_custom_call" | custom-call | tf_op jit(solution)/shard_map/probs/pallas_call | solution.py:193
  76.8 2.1 %collective-permute-done.10 = bf16[2,256,512]{2,1,0:T(8,128)(2,1)S(1)} collective-permute-done((bf16[2,256,512]{2,1,0:T(8,128)(2,1)}, bf16[2,256,512]{2,1,0:T(8,128)(2,1)S(1)}, u32[]{:S(2)}, u32[]{:S(2)}) %collective-permute-start.10) | collective-permute-done | bytes 524320 | tf_op jit(solution)/shard_map/ppermute | solution.py:33
  80.4 10.0 %split.1 = (bf16[2048,256]{1,0:T(8,128)(2,1)}, bf16[2048,256]{1,0:T(8,128)(2,1)}) custom-call(s32[2]{0:T(128)} %pad_add_fusion.where_ref, bf16[256,4096]{1,0:T(8,128)(2,1)} %bitcast.39), custom_call_target="tpu_custom_call" | custom-call | tf_op jit(solution)/shard_map/split/pallas_call | solution.py:247
  92.3 2.7 %collective-permute-start.12 = (bf16[256,512]{1,0:T(8,128)(2,1)S(1)}, bf16[256,512]{1,0:T(8,128)(2,1)S(1)}, u32[]{:S(2)}, u32[]{:S(2)}) collective-permute-start(bf16[256,512]{1,0:T(8,128)(2,1)S(1)} %add_convert_fusion.1), channel_id=1, source_target_pairs={{16,0},{24,8},{32,16},{40,24},{48,32},{56,40},{64,48},{72,56},{80,... | collective-permute-start | bytes 786440 | tf_op jit(solution)/shard_map/ppermute | solution.py:29
  95.0 8.3 %collective-permute-done.12 = bf16[256,512]{1,0:T(8,128)(2,1)S(1)} collective-permute-done((bf16[256,512]{1,0:T(8,128)(2,1)S(1)}, bf16[256,512]{1,0:T(8,128)(2,1)S(1)}, u32[]{:S(2)}, u32[]{:S(2)}) %collective-permute-start.12) | collective-permute-done | bytes 262176 | tf_op jit(solution)/shard_map/ppermute | solution.py:29
  104.6 1.5 collective-permute-done.14.vb_ref
  106.8 4.7 %weight_grad.1 = bf16[4,4,8,16,512]{4,3,2,1,0:T(8,128)(2,1)} custom-call(bf16[2048,256]{1,0:T(8,128)(2,1)} %get-tuple-element.22.xa_ref, bf16[2048,256]{1,0:T(8,128)(2,1)} %collective-permute-done.13.xb_ref, bf16[256,512]{1,0:T(8,128)(2,1)} %copy-done.4, bf16[256,512]{1,0:T(8,128)(2,1)} %copy-done.11), custom_call_target="tpu_custom_call" | custom-call | tf_op jit(solution)/shard_map/weight_grad/pallas_call | solution.py:351
  111.6 8.2 %all-to-all-start.1 = ((bf16[16,128,512]{2,1,0:T(8,128)(2,1)}), bf16[16,128,512]{2,1,0:T(8,128)(2,1)}, u32[]{:S(2)}, u32[]{:S(2)}) async-start(bf16[16,128,512]{2,1,0:T(8,128)(2,1)} %bitcast.41), calls=%async_computation.1 | async-start | bytes 4194304 | tf_op jit(solution)/shard_map/all_to_all | solution.py:362
  119.7 5.0 %values.1.v0 = bf16[256,512]{1,0:T(8,128)(2,1)} custom-call(s32[2]{0:T(128)} %pad_add_fusion.where_ref, bf16[256,4096]{1,0:T(8,128)(2,1)} %bitcast.40, bf16[4096,256]{1,0:T(8,128)(2,1)} %bitcast.37, bf16[4096,256]{1,0:T(8,128)(2,1)} %collective-permute-done.3.wb_ref), custom_call_target="tpu_custom_call" | custom-call | tf_op jit(solution)/shard_map/values/pallas_call | solution.py:289
  124.8 5.1 %collective-permute-start.4 = (bf16[256,512]{1,0:T(8,128)(2,1)}, bf16[256,512]{1,0:T(8,128)(2,1)S(1)}, u32[]{:S(2)}, u32[]{:S(2)}) collective-permute-start(bf16[256,512]{1,0:T(8,128)(2,1)} %values.1.v0), channel_id=1, source_target_pairs={{0,16},{8,24},{16,32},{24,40},{32,48},{40,56},{48,64},{56,72},{64,... | collective-permute-start | bytes 786440 | tf_op jit(solution)/shard_map/ppermute | solution.py:29
  129.8 9.7 %collective-permute-done.4.v2 = bf16[256,512]{1,0:T(8,128)(2,1)S(1)} collective-permute-done((bf16[256,512]{1,0:T(8,128)(2,1)}, bf16[256,512]{1,0:T(8,128)(2,1)S(1)}, u32[]{:S(2)}, u32[]{:S(2)}) %collective-permute-start.4) | collective-permute-done | bytes 262176 | tf_op jit(solution)/shard_map/ppermute | solution.py:29
  142.0 9.5 %collective-permute-done.5.v3 = bf16[256,512]{1,0:T(8,128)(2,1)S(1)} collective-permute-done((bf16[256,512]{1,0:T(8,128)(2,1)S(1)}, bf16[256,512]{1,0:T(8,128)(2,1)S(1)}, u32[]{:S(2)}, u32[]{:S(2)}) %collective-permute-start.5) | collective-permute-done | bytes 262176 | tf_op jit(solution)/shard_map/ppermute | solution.py:29
  152.4 14.6 %grads.1 = (bf16[256,2048]{1,0:T(8,128)(2,1)}, f32[256,512]{1,0:T(8,128)}, f32[256,512]{1,0:T(8,128)}, bf16[2,256,512]{2,1,0:T(8,128)(2,1)}) custom-call(s32[2]{0:T(128)} %pad_add_fusion.where_ref, s32[1,32]{1,0:T(1,128)} %lens_ref.3, s32[1,32]{1,0:T(1,128)} %order_ref.3, bf16[256,2048]{1,0:T(8,128)(2,1)} %bitcast.43, bf16[256,2048]{1,0:T(8,128)(2,1)} %bitcast.45, ...), custom_call_target="tpu_custom_call" | custom-call | tf_op jit(solution)/shard_map/grads/pallas_call | solution.py:210
  167.1 2.1 %collective-permute-done.7 = bf16[2,256,512]{2,1,0:T(8,128)(2,1)S(1)} collective-permute-done((bf16[2,256,512]{2,1,0:T(8,128)(2,1)}, bf16[2,256,512]{2,1,0:T(8,128)(2,1)S(1)}, u32[]{:S(2)}, u32[]{:S(2)}) %collective-permute-start.7) | collective-permute-done | bytes 524320 | tf_op jit(solution)/shard_map/ppermute | solution.py:33
  170.0 2.6 %reduce_sum.21 = bf16[128,512]{1,0:T(8,128)(2,1)} reduce(bf16[16,128,512]{2,1,0:T(8,128)(2,1)} %all-to-all-done.1, bf16[]{:T(256)} %constant.28.clone.1), dimensions={0}, to_apply=%region_0.1 | reduce | flops 983040 | bytes 2228226 | tf_op jit(solution)/shard_map/reduce_sum | solution.py:391
  172.5 3.4 %all-to-all-start.2 = ((bf16[8,16,512]{2,1,0:T(8,128)(2,1)}), bf16[8,16,512]{2,1,0:T(8,128)(2,1)S(1)}, u32[]{:S(2)}, u32[]{:S(2)}) async-start(bf16[8,16,512]{2,1,0:T(8,128)(2,1)} %bitcast.18), calls=%async_computation.2 | async-start | bytes 262144 | tf_op jit(solution)/shard_map/all_to_all | solution.py:362
  176.1 4.4 %collective-permute-start.9 = (bf16[256,512]{1,0:T(8,128)(2,1)S(1)}, bf16[256,512]{1,0:T(8,128)(2,1)S(1)}, u32[]{:S(2)}, u32[]{:S(2)}) collective-permute-start(bf16[256,512]{1,0:T(8,128)(2,1)S(1)} %add_convert_fusion.3), channel_id=1, source_target_pairs={{16,0},{24,8},{32,16},{40,24},{48,32},{56,40},{64,48},{72,56},{80,... | collective-permute-start | bytes 786440 | tf_op jit(solution)/shard_map/ppermute | solution.py:29
  180.5 4.9 %all-to-all-done.2 = bf16[8,16,512]{2,1,0:T(8,128)(2,1)S(1)} async-done(((bf16[8,16,512]{2,1,0:T(8,128)(2,1)}), bf16[8,16,512]{2,1,0:T(8,128)(2,1)S(1)}, u32[]{:S(2)}, u32[]{:S(2)}) %all-to-all-start.2) | async-done | bytes 131104 | tf_op jit(solution)/shard_map/all_to_all | solution.py:362
  186.1 5.2 %input_grad.1 = bf16[256,4096]{1,0:T(8,128)(2,1)} custom-call(s32[2]{0:T(128)} %pad_add_fusion.where_ref, bf16[256,512]{1,0:T(8,128)(2,1)} %copy-done.4, bf16[4096,256]{1,0:T(8,128)(2,1)} %bitcast.38, bf16[4096,256]{1,0:T(8,128)(2,1)} %collective-permute-done.3.wb_ref), custom_call_target="tpu_custom_call" | custom-call | tf_op jit(solution)/shard_map/input_grad/pallas_call | solution.py:324
  191.2 3.3 %collective-permute-done.9 = bf16[256,512]{1,0:T(8,128)(2,1)S(1)} collective-permute-done((bf16[256,512]{1,0:T(8,128)(2,1)S(1)}, bf16[256,512]{1,0:T(8,128)(2,1)S(1)}, u32[]{:S(2)}, u32[]{:S(2)}) %collective-permute-start.9) | collective-permute-done | bytes 262176 | tf_op jit(solution)/shard_map/ppermute | solution.py:29
  (55 shorter events, 18.5 us)
Async XLA Ops:
  3.2 6.0 %copy-start.2 = (bf16[1,256,512]{2,1,0:T(8,128)(2,1)S(1)}, bf16[1,256,512]{2,1,0:T(8,128)(2,1)}, u32[]{:S(2)}) copy-start(bf16[1,256,512]{2,1,0:T(8,128)(2,1)} %param.9) | copy-start | bytes 786436
  3.2 50.7 %all-to-all-start = ((bf16[8,512,256]{2,1,0:T(8,128)(2,1)}), bf16[8,512,256]{2,1,0:T(8,128)(2,1)S(1)}, u32[]{:S(2)}, u32[]{:S(2)}) async-start(bf16[8,512,256]{2,1,0:T(8,128)(2,1)} %broadcast_in_dim.15), calls=%async_computation | async-start | bytes 4194304 | tf_op jit(solution)/shard_map/all_to_all | solution.py:362
  9.1 42.6 %collective-permute-start = (bf16[256,512]{1,0:T(8,128)(2,1)S(1)}, bf16[256,512]{1,0:T(8,128)(2,1)S(1)}, u32[]{:S(2)}, u32[]{:S(2)}) collective-permute-start(bf16[256,512]{1,0:T(8,128)(2,1)S(1)} %bitcast.48), channel_id=1, source_target_pairs={{0,16},{8,24},{16,32},{24,40},{32,48},{40,56},{48,64},{56,72},{64,... | collective-permute-start | bytes 786440 | tf_op jit(solution)/shard_map/ppermute | solution.py:29
  51.7 11.7 %copy-start.3 = (bf16[256,512]{1,0:T(8,128)(2,1)}, bf16[256,512]{1,0:T(8,128)(2,1)S(1)}, u32[]{:S(2)}) copy-start(bf16[256,512]{1,0:T(8,128)(2,1)S(1)} %collective-permute-done.k2) | copy-start | bytes 786436
  52.6 10.8 %collective-permute-start.2 = (bf16[2,256,512]{2,1,0:T(8,128)(2,1)}, bf16[2,256,512]{2,1,0:T(8,128)(2,1)S(1)}, u32[]{:S(2)}, u32[]{:S(2)}) collective-permute-start(bf16[2,256,512]{2,1,0:T(8,128)(2,1)} %pad_maximum_fusion), channel_id=1, source_target_pairs={{0,8},{8,0},{1,9},{9,1},{2,10},{10,2},{3,11},{11,3},{4,12},{12,4},... | collective-permute-start | bytes 1572872 | tf_op jit(solution)/shard_map/ppermute | solution.py:33
  52.6 10.8 %collective-permute-start.1 = (bf16[256,512]{1,0:T(8,128)(2,1)S(1)}, bf16[256,512]{1,0:T(8,128)(2,1)}, u32[]{:S(2)}, u32[]{:S(2)}) collective-permute-start(bf16[256,512]{1,0:T(8,128)(2,1)S(1)} %collective-permute-done.k2), channel_id=1, source_target_pairs={{8,16},{24,32},{40,48},{56,64},{72,80},{88,96},{104,112},{120,128}... | collective-permute-start | bytes 786440 | tf_op jit(solution)/shard_map/ppermute | solution.py:29
  53.9 36.4 %copy-start.1 = (bf16[8,512,256]{2,1,0:T(8,128)(2,1)}, bf16[8,512,256]{2,1,0:T(8,128)(2,1)S(1)}, u32[]{:S(2)}) copy-start(bf16[8,512,256]{2,1,0:T(8,128)(2,1)S(1)} %all-to-all-done) | copy-start | bytes 6291460
  53.9 65.8 %collective-permute-start.3 = (bf16[4096,256]{1,0:T(8,128)(2,1)S(1)}, bf16[4096,256]{1,0:T(8,128)(2,1)}, u32[]{:S(2)}, u32[]{:S(2)}) collective-permute-start(bf16[4096,256]{1,0:T(8,128)(2,1)S(1)} %bitcast.36), channel_id=1, source_target_pairs={{0,8},{8,0},{1,9},{9,1},{2,10},{10,2},{3,11},{11,3},{4,12},{12,4},... | collective-permute-start | bytes 6291464 | tf_op jit(solution)/shard_map/ppermute | solution.py:33
  76.7 2.2 %collective-permute-start.10 = (bf16[2,256,512]{2,1,0:T(8,128)(2,1)}, bf16[2,256,512]{2,1,0:T(8,128)(2,1)S(1)}, u32[]{:S(2)}, u32[]{:S(2)}) collective-permute-start(bf16[2,256,512]{2,1,0:T(8,128)(2,1)} %get-tuple-element.20), channel_id=1, source_target_pairs={{0,8},{8,0},{1,9},{9,1},{2,10},{10,2},{3,11},{11,3},{4,12},{12,4},... | collective-permute-start | bytes 1572872 | tf_op jit(solution)/shard_map/ppermute | solution.py:33
  79.0 12.1 %collective-permute-start.11 = (bf16[256,512]{1,0:T(8,128)(2,1)S(1)}, bf16[256,512]{1,0:T(8,128)(2,1)}, u32[]{:S(2)}, u32[]{:S(2)}) collective-permute-start(bf16[256,512]{1,0:T(8,128)(2,1)S(1)} %slice_bitcast_fusion), channel_id=1, source_target_pairs={{24,8},{40,24},{56,40},{72,56},{88,72},{104,88},{120,104},{136,120... | collective-permute-start | bytes 786440 | tf_op jit(solution)/shard_map/ppermute | solution.py:29
  90.3 14.3 %collective-permute-start.13 = (bf16[2048,256]{1,0:T(8,128)(2,1)}, bf16[2048,256]{1,0:T(8,128)(2,1)}, u32[]{:S(2)}, u32[]{:S(2)}) collective-permute-start(bf16[2048,256]{1,0:T(8,128)(2,1)} %get-tuple-element.23), channel_id=1, source_target_pairs={{0,8},{8,0},{1,9},{9,1},{2,10},{10,2},{3,11},{11,3},{4,12},{12,4},... | collective-permute-start | bytes 3145736 | tf_op jit(solution)/shard_map/ppermute | solution.py:33
  92.3 11.0 %collective-permute-start.12 = (bf16[256,512]{1,0:T(8,128)(2,1)S(1)}, bf16[256,512]{1,0:T(8,128)(2,1)S(1)}, u32[]{:S(2)}, u32[]{:S(2)}) collective-permute-start(bf16[256,512]{1,0:T(8,128)(2,1)S(1)} %add_convert_fusion.1), channel_id=1, source_target_pairs={{16,0},{24,8},{32,16},{40,24},{48,32},{56,40},{64,48},{72,56},{80,... | collective-permute-start | bytes 786440 | tf_op jit(solution)/shard_map/ppermute | solution.py:29
  104.5 1.6 collective-permute-start.14
  111.6 58.4 %all-to-all-start.1 = ((bf16[16,128,512]{2,1,0:T(8,128)(2,1)}), bf16[16,128,512]{2,1,0:T(8,128)(2,1)}, u32[]{:S(2)}, u32[]{:S(2)}) async-start(bf16[16,128,512]{2,1,0:T(8,128)(2,1)} %bitcast.41), calls=%async_computation.1 | async-start | bytes 4194304 | tf_op jit(solution)/shard_map/all_to_all | solution.py:362
  124.8 14.8 %collective-permute-start.4 = (bf16[256,512]{1,0:T(8,128)(2,1)}, bf16[256,512]{1,0:T(8,128)(2,1)S(1)}, u32[]{:S(2)}, u32[]{:S(2)}) collective-permute-start(bf16[256,512]{1,0:T(8,128)(2,1)} %values.1.v0), channel_id=1, source_target_pairs={{0,16},{8,24},{16,32},{24,40},{32,48},{40,56},{48,64},{56,72},{64,... | collective-permute-start | bytes 786440 | tf_op jit(solution)/shard_map/ppermute | solution.py:29
  139.5 12.0 %copy-start.6 = (bf16[256,512]{1,0:T(8,128)(2,1)}, bf16[256,512]{1,0:T(8,128)(2,1)S(1)}, u32[]{:S(2)}) copy-start(bf16[256,512]{1,0:T(8,128)(2,1)S(1)} %collective-permute-done.4.v2) | copy-start | bytes 786436
  140.6 10.9 %collective-permute-start.6 = (bf16[2,256,512]{2,1,0:T(8,128)(2,1)S(1)}, bf16[2,256,512]{2,1,0:T(8,128)(2,1)S(1)}, u32[]{:S(2)}, u32[]{:S(2)}) collective-permute-start(bf16[2,256,512]{2,1,0:T(8,128)(2,1)S(1)} %pad_maximum_fusion.1), channel_id=1, source_target_pairs={{0,8},{8,0},{1,9},{9,1},{2,10},{10,2},{3,11},{11,3},{4,12},{12,4},... | collective-permute-start | bytes 1572872 | tf_op jit(solution)/shard_map/ppermute | solution.py:33
  140.7 10.8 %collective-permute-start.5 = (bf16[256,512]{1,0:T(8,128)(2,1)S(1)}, bf16[256,512]{1,0:T(8,128)(2,1)S(1)}, u32[]{:S(2)}, u32[]{:S(2)}) collective-permute-start(bf16[256,512]{1,0:T(8,128)(2,1)S(1)} %collective-permute-done.4.v2), channel_id=1, source_target_pairs={{8,16},{24,32},{40,48},{56,64},{72,80},{88,96},{104,112},{120,128}... | collective-permute-start | bytes 786440 | tf_op jit(solution)/shard_map/ppermute | solution.py:29
  167.0 8.9 %copy-start.8 = (f32[256,512]{1,0:T(8,128)S(1)}, f32[256,512]{1,0:T(8,128)}, u32[]{:S(2)}) copy-start(f32[256,512]{1,0:T(8,128)} %get-tuple-element.18) | copy-start | bytes 1572868
  167.0 2.2 %collective-permute-start.7 = (bf16[2,256,512]{2,1,0:T(8,128)(2,1)}, bf16[2,256,512]{2,1,0:T(8,128)(2,1)S(1)}, u32[]{:S(2)}, u32[]{:S(2)}) collective-permute-start(bf16[2,256,512]{2,1,0:T(8,128)(2,1)} %get-tuple-element.17), channel_id=1, source_target_pairs={{0,8},{8,0},{1,9},{9,1},{2,10},{10,2},{3,11},{11,3},{4,12},{12,4},... | collective-permute-start | bytes 1572872 | tf_op jit(solution)/shard_map/ppermute | solution.py:33
  169.3 6.7 %collective-permute-start.8 = (bf16[256,512]{1,0:T(8,128)(2,1)S(1)}, bf16[256,512]{1,0:T(8,128)(2,1)S(1)}, u32[]{:S(2)}, u32[]{:S(2)}) collective-permute-start(bf16[256,512]{1,0:T(8,128)(2,1)S(1)} %slice_bitcast_fusion.2), channel_id=1, source_target_pairs={{24,8},{40,24},{56,40},{72,56},{88,72},{104,88},{120,104},{136,120... | collective-permute-start | bytes 786440 | tf_op jit(solution)/shard_map/ppermute | solution.py:29
  172.5 12.9 %all-to-all-start.2 = ((bf16[8,16,512]{2,1,0:T(8,128)(2,1)}), bf16[8,16,512]{2,1,0:T(8,128)(2,1)S(1)}, u32[]{:S(2)}, u32[]{:S(2)}) async-start(bf16[8,16,512]{2,1,0:T(8,128)(2,1)} %bitcast.18), calls=%async_computation.2 | async-start | bytes 262144 | tf_op jit(solution)/shard_map/all_to_all | solution.py:362
  176.1 18.5 %collective-permute-start.9 = (bf16[256,512]{1,0:T(8,128)(2,1)S(1)}, bf16[256,512]{1,0:T(8,128)(2,1)S(1)}, u32[]{:S(2)}, u32[]{:S(2)}) collective-permute-start(bf16[256,512]{1,0:T(8,128)(2,1)S(1)} %add_convert_fusion.3), channel_id=1, source_target_pairs={{16,0},{24,8},{32,16},{40,24},{48,32},{56,40},{64,48},{72,56},{80,... | collective-permute-start | bytes 786440 | tf_op jit(solution)/shard_map/ppermute | solution.py:29
  186.1 8.5 %copy-start.7 = (f32[256,512]{1,0:T(8,128)S(1)}, f32[256,512]{1,0:T(8,128)}, u32[]{:S(2)}) copy-start(f32[256,512]{1,0:T(8,128)} %get-tuple-element.16) | copy-start | bytes 1572868
  (6 other events, 5.8 us)
